TPU v7x, 8 devices: a whole 2x2x1 slice. The times are simulated.
8 devices in a mesh: batch: 1 (over z), cy: 2 (over y), cx: 4 (over x, core).
Axes of the slice: x: 2, y: 2, z: 1, core: 2. Of those that a mesh axis runs over, the one named last changes fastest.
Arguments:
- q: bfloat16 [1536, 64, 128], P(('batch', 'cy', 'cx'))
- k: bfloat16 [1536, 8, 128], P(('batch', 'cy', 'cx'))
- v: bfloat16 [1536, 8, 128], P(('batch', 'cy', 'cx'))
Outputs:
- output: bfloat16 [1536, 64, 128], P(('batch', 'cy', 'cx'))
All inputs are finite; a program needn't handle non-finite values.
Results may differ from a plain program's by a relative error of at most 0.00212845.
Values are sent between devices in bfloat16 or wider.
A program may use at most 1 GiB of HBM per device.

v0:
```python
import functools
import math

import jax
import jax.numpy as jnp
from jax import lax
from jax.experimental import pallas as pl
from jax.experimental.pallas import tpu as pltpu
from jax.sharding import PartitionSpec as P

MESH = pl.DeviceIdType.MESH
AHEAD = 2
QT = 32
NT = 3
NEG = -jnp.inf


def chunks_of(chip):
    far = 3 - chip
    early_low = [(0, j) for j in range(chip + 1) if j != far]
    late_low = [(0, far)] if far <= chip else []
    early_high = early_low + [(0, j) for j in range(chip + 1, 4) if j != far]
    early_high += [(1, j) for j in range(3, chip - 1, -1) if j != far]
    late_high = [(0, far)] + ([(1, far)] if far >= chip else [])
    return early_high, early_low, late_high, late_low


def kernel(q_hbm, k_hbm, v_hbm, o_ref, q_last, kv_last, mk, lk, acck, q_s, raw, f32s, kv, vte, vtl, *rest,
           scale):
    s_s, p_s, m_s, al_s, be_s, l_s = (rest[3 * i:3 * i + 3] for i in range(6))
    load_sem, send_sem, xy_sem, dg_sem, se_sem, sl_sem = rest[18:]
    G, T, GQ, D = q_s.shape
    CH = T // 2
    C2 = 2 * CH
    W = QT * GQ
    cb = lax.axis_index('batch')
    cy = lax.axis_index('cy')
    cx = lax.axis_index('cx')
    ox = lax.rem(cx + 2, 4)
    sx = cx + 1 - 2 * lax.rem(cx, 2)
    oy = 1 - cy
    x_dev = (cb, cy, ox)
    y_dev = (cb, oy, cx)
    s_dev = (cb, cy, sx)
    me = cy * 4 + cx
    rx, ry, rd = cy * 4 + ox, oy * 4 + cx, oy * 4 + ox
    odd = lax.rem(cx, 2)
    chip_of = me // 2

    kcopy = pltpu.make_async_copy(k_hbm, raw.at[0], load_sem.at[0])
    vcopy = pltpu.make_async_copy(v_hbm, raw.at[1], load_sem.at[1])
    kcopy.start()
    vcopy.start()

    barrier = pltpu.get_barrier_semaphore()
    for dev in (x_dev, y_dev, s_dev):
        pl.semaphore_signal(barrier, inc=1, device_id=dev, device_id_type=MESH)

    for g in range(G):
        pltpu.make_async_copy(q_hbm.at[:, g], q_s.at[g], load_sem.at[2]).start()

    def take(g):
        for which in (0, 1):
            rows = f32s[which, pl.ds(g, T, stride=G), :].astype(jnp.bfloat16)
            kv[g, 2 * me, which] = rows[:CH]
            kv[g, 2 * me + 1, which] = rows[CH:]

    for which, copy in ((0, kcopy), (1, vcopy)):
        copy.wait()
        f32s[which] = raw[which].astype(jnp.float32).reshape(T * G, D)
    for g in range(AHEAD):
        take(g)

    pl.semaphore_wait(barrier, 3)

    def piece(g, r, full):
        return kv.at[g, pl.ds(2 * r, 2)] if full else kv.at[g, 2 * r]

    def send(g, ref, recv_sem, dev):
        pltpu.make_async_remote_copy(
            src_ref=ref, dst_ref=ref, send_sem=send_sem.at[g], recv_sem=recv_sem.at[g],
            device_id=dev, device_id_type=MESH).start()

    def arrived(g, count, recv_sem):
        ref = kv.at[g, 0:count]
        pltpu.make_async_remote_copy(
            src_ref=ref, dst_ref=ref, send_sem=send_sem.at[g], recv_sem=recv_sem.at[g],
            device_id=x_dev, device_id_type=MESH).wait_recv()

    c2 = scale * math.log2(math.e)
    sub = lax.broadcasted_iota(jnp.int32, (8, W), 0)
    base = sub - lax.broadcasted_iota(jnp.int32, (8, W), 1) // GQ

    def keys(g, chunk_list, which):
        parts = [kv[g, 4 * j + half + 2 * core, which] for half, j in chunk_list for core in (0, 1)]
        return jnp.concatenate(parts, axis=0)

    def pipeline(chip):
        xc, yc, far = chip ^ 1, chip ^ 2, chip ^ 3
        own_x, own_y = True, True
        got_x, got_y, got_far = True, True, True
        cross_high = True
        n_xy = 2 + got_x + got_y
        n_far = 1 + got_far
        n_sent = (2 + own_x + own_y) + 2 + (1 + cross_high) + (2 + got_x + got_y) + n_far

        def start_own(g):
            send(g, piece(g, me, own_x), xy_sem, x_dev)
            send(g, piece(g, me, own_y), xy_sem, y_dev)
            send(g, piece(g, me, True), se_sem, s_dev)

        def forward(g):
            arrived(g, n_xy, xy_sem)
            send(g, kv.at[g, 2 * rx], dg_sem, y_dev)
            if cross_high:
                send(g, kv.at[g, 2 * ry + 1], dg_sem, x_dev)
            send(g, piece(g, rx, got_x), se_sem, s_dev)
            send(g, piece(g, ry, got_y), se_sem, s_dev)

        def diagonal(g):
            arrived(g, n_far, dg_sem)
            send(g, piece(g, rd, got_far), sl_sem, s_dev)

        for g in range(AHEAD):
            start_own(g)
        for g in range(AHEAD, G):
            take(g)
        pltpu.make_async_copy(q_s, q_s, load_sem.at[2]).wait()
        q_last[...] = q_s[G - 1]

        lists = chunks_of(chip)
        names = ('eh', 'el', 'lh', 'll')
        rows = {}
        at = 0
        for name, lst in zip(names, lists):
            rows[name] = (at, C2 * len(lst))
            at += C2 * len(lst)
        lst = dict(zip(names, lists))
        halves = (1, 0)

        def transposed(g, slot, names):
            for name, ref in names:
                n = rows[name][1]
                ref[slot, :, :n] = keys(g, lst[name], 1).T

        def split(u):
            return lax.div(u + NT, NT) - 1, lax.rem(u + NT, NT)

        def score(g, t, half, name, slot, masked):
            at, n = rows[name]
            qv = q_s[g, pl.ds(half * CH + t * QT, QT)].reshape(W, D)
            s = lax.dot_general(keys(g, lst[name], 0), qv, (((1,), (1,)), ((), ())),
                                preferred_element_type=jnp.float32)
            edge = n - C2 if masked else n
            top = None
            if edge:
                s_s[slot][at:at + edge] = s[:edge]
                for i in range(edge // 8):
                    si = s[8 * i:8 * i + 8]
                    top = si if top is None else jnp.maximum(top, si)
            if masked:
                thr = t * QT + CH * (odd if half == 0 else -odd)
                for i in range(C2 // 8):
                    first = 8 * i if (half == 0 or i < CH // 8) else 8 * i - C2
                    si = jnp.where(base <= thr - first, s[edge + 8 * i:edge + 8 * i + 8], NEG)
                    s_s[slot][at + edge + 8 * i:at + edge + 8 * i + 8] = si
                    top = si if top is None else jnp.maximum(top, si)
            return jnp.max(top, axis=0, keepdims=True)

        def stage_a(u, slot, early=True, late=True):
            g, t = split(u)
            gl = jnp.where(g == 0, G, g - 1)
            ql = jnp.maximum(g - 1, 0)
            for half in halves:
                e, l = ('eh', 'lh') if half else ('el', 'll')
                if late and lst[l]:
                    old = mk[half, t]
                    m = jnp.maximum(score_late(gl, ql, t, half, l, slot), old)
                    m_s[slot][2 + half] = m
                    al_s[slot][half] = jnp.exp2((old - m) * c2)
                if early:
                    m = score(g, t, half, e, slot, True)
                    m_s[slot][half] = m
                    mk[half, t] = m

        def score_late(gl, ql, t, half, name, slot):
            at, n = rows[name]
            qv = q_s[ql, pl.ds(half * CH + t * QT, QT)].reshape(W, D)
            s = lax.dot_general(keys(gl, lst[name], 0), qv, (((1,), (1,)), ((), ())),
                                preferred_element_type=jnp.float32)
            s_s[slot][at:at + n] = s
            top = s[:8]
            for i in range(1, n // 8):
                top = jnp.maximum(top, s[8 * i:8 * i + 8])
            return jnp.max(top, axis=0, keepdims=True)

        def weights(name, slot, m):
            at, n = rows[name]
            total = None
            for j in range(n // C2):
                sl = slice(at + j * C2, at + (j + 1) * C2)
                p = jnp.exp2((s_s[slot][sl] - m) * c2)
                for i in range(C2 // 8):
                    pi = p[8 * i:8 * i + 8]
                    total = pi if total is None else total + pi
                p_s[slot][sl] = p.astype(jnp.bfloat16)
            return jnp.sum(total, axis=0, keepdims=True)

        def stage_b(u, slot, early=True, late=True):
            g, t = split(u)
            for half in halves:
                e, l = ('eh', 'lh') if half else ('el', 'll')
                if late and lst[l]:
                    total = weights(l, slot, m_s[slot][2 + half])
                    l_s[slot][2 + half] = lk[half, t] * al_s[slot][half] + total
                    be_s[slot][half] = al_s[slot][half]
                if early:
                    total = weights(e, slot, m_s[slot][half])
                    l_s[slot][half] = total
                    lk[half, t] = total

        def values(name, ref, par, slot):
            at, n = rows[name]
            return lax.dot_general(ref[par, :, :n], p_s[slot][at:at + n], (((1,), (0,)), ((), ())),
                                   preferred_element_type=jnp.float32)

        def put(g, t, half, acc, total):
            out = (acc * (1.0 / total)).astype(jnp.bfloat16).T
            o_ref[pl.ds(half * CH + t * QT, QT), g] = out.reshape(QT, GQ, D)

        def stage_c(u, slot, early=True, late=True):
            g, t = split(u)
            ge = jnp.maximum(g, 0)
            gl = jnp.maximum(g - 1, 0)
            for half in halves:
                e, l = ('eh', 'lh') if half else ('el', 'll')
                if late and lst[l]:
                    acc = acck[half, t] * be_s[slot][half] + values(l, vtl, lax.rem(gl, 2), slot)
                    put(gl, t, half, acc, l_s[slot][2 + half])
                if early:
                    acc = values(e, vte, lax.rem(ge, 2), slot)
                    if lst[l]:
                        acck[half, t] = acc
                    else:
                        put(ge, t, half, acc, l_s[slot][half])

        def service(g):
            @pl.when(g < G - 1)
            def _():
                forward(g + 1)

            arrived(g, 2 + n_xy, se_sem)

            @pl.when(g > 0)
            def _():
                arrived(g - 1, n_far, sl_sem)
                transposed(g - 1, lax.rem(g - 1, 2), (('lh', vtl),))
            transposed(g, lax.rem(g, 2), (('eh', vte),))

        n = NT * G
        forward(0)
        start_own(AHEAD)

        def body(pair, carry):
            for odd_i in (0, 1):
                i = 2 * pair + odd_i

                @pl.when(lax.rem(i, NT) == 0)
                def _(i=i):
                    service(lax.div(i, NT))

                @pl.when(jnp.logical_and(lax.rem(i, NT) == 1, i < n - NT - NT * AHEAD))
                def _(i=i):
                    start_own(lax.div(i, NT) + 1 + AHEAD)

                @pl.when(jnp.logical_and(lax.rem(i, NT) == 1, i < n - NT))
                def _(i=i):
                    diagonal(lax.div(i, NT))

                stage_a(i, odd_i)
                stage_b(i - 1, 1 - odd_i)
                stage_c(i - 1, 1 - odd_i)
            return carry

        lax.fori_loop(0, n // 2, body, 0)
        stage_b(n - 1, 1 - n % 2)
        stage_c(n - 1, 1 - n % 2)

        diagonal(G - 1)
        arrived(G - 1, n_far, sl_sem)
        for i, (half, j) in enumerate(lst['lh']):
            for core in (0, 1):
                kv_last[2 * i + core] = kv[G - 1, 4 * j + half + 2 * core]

        def drain(g, carry):
            ref = kv.at[g, 0:n_sent]
            pltpu.make_async_remote_copy(
                src_ref=ref, dst_ref=ref, send_sem=send_sem.at[g], recv_sem=xy_sem.at[g],
                device_id=x_dev, device_id_type=MESH).wait_send()
            return carry

        lax.fori_loop(0, G, drain, 0)

    def tail(stage_a, stage_b, stage_c, n):
        for t in range(NT):
            stage_a(n + t, t, early=False)
        for t in range(NT):
            stage_b(n + t, t, early=False)
        for t in range(NT):
            stage_c(n + t, t, early=False)

    for chip in range(4):
        @pl.when(chip_of == chip)
        def _(chip=chip):
            pipeline(chip)


def last_kernel(o_part, q_last, kv_last, mk, lk, acck, o_hbm, out_s, s_s, p_s, sem, *, scale):
    T, G, GQ, D = o_part.shape
    CH = T // 2
    W = QT * GQ
    chip_of = lax.axis_index('cy') * 2 + lax.axis_index('cx') // 2
    step = T // 4
    copies = [pltpu.make_async_copy(o_part.at[pl.ds(i * step, step), pl.ds(0, G - 1)],
                                    o_hbm.at[pl.ds(i * step, step), pl.ds(0, G - 1)], sem.at[i]) for i in range(4)]
    for c in copies:
        c.start()
    c2 = scale * math.log2(math.e)

    def merge(chip):
        late_high, late_low = chunks_of(chip)[2:]
        tiles = [(1, t, len(late_high)) for t in range(NT)]
        tiles += [(0, t, len(late_low)) for t in range(NT) if late_low]
        ends = []
        if not late_low:
            ends.append(pltpu.make_async_copy(o_part.at[pl.ds(0, CH), G - 1], o_hbm.at[pl.ds(0, CH), G - 1], sem.at[G]))
            ends[0].start()
        n_pieces = 2 * len(late_high)
        keys = kv_last[0:n_pieces, 0].reshape(n_pieces * CH, D)
        vals = kv_last[0:n_pieces, 1].reshape(n_pieces * CH, D).T
        slabs = lambda x: [x[8 * i:8 * i + 8] for i in range(x.shape[0] // 8)]
        tops, sums, at = [], [], 0
        for half, t, count in tiles:
            n = 2 * CH * count
            rows = slice(half * CH + t * QT, half * CH + (t + 1) * QT)
            s = lax.dot_general(keys[:n], q_last[rows].reshape(W, D), (((1,), (1,)), ((), ())),
                                preferred_element_type=jnp.float32)
            s_s[at:at + n] = s
            top = functools.reduce(jnp.maximum, slabs(s))
            tops.append(jnp.maximum(jnp.max(top, axis=0, keepdims=True), mk[half, t]))
            at += n
        at = 0
        for (half, t, count), m in zip(tiles, tops):
            n = 2 * CH * count
            total = None
            for j in range(count):
                sl = slice(at + j * 2 * CH, at + (j + 1) * 2 * CH)
                p = jnp.exp2((s_s[sl] - m) * c2)
                part = functools.reduce(jnp.add, slabs(p))
                total = part if total is None else total + part
                p_s[sl] = p.astype(jnp.bfloat16)
            sums.append(jnp.sum(total, axis=0, keepdims=True))
            at += n
        at = 0
        for (half, t, count), m, total in zip(tiles, tops, sums):
            n = 2 * CH * count
            rows = slice(half * CH + t * QT, half * CH + (t + 1) * QT)
            alpha = jnp.exp2((mk[half, t] - m) * c2)
            inv = 1.0 / (lk[half, t] * alpha + total)
            acc = acck[half, t] * (alpha * inv) + lax.dot_general(
                vals[:, :n], p_s[at:at + n], (((1,), (0,)), ((), ())), preferred_element_type=jnp.float32) * inv
            out_s[rows] = acc.astype(jnp.bfloat16).T.reshape(QT, GQ, D)
            at += n
        for half in ((1, 0) if late_low else (1,)):
            ends.append(pltpu.make_async_copy(
                out_s.at[pl.ds(half * CH, CH)], o_hbm.at[pl.ds(half * CH, CH), G - 1], sem.at[G + 1 + half]))
            ends[-1].start()
        for c in ends:
            c.wait()

    for chip in range(4):
        @pl.when(chip_of == chip)
        def _(chip=chip):
            merge(chip)

    for c in copies:
        c.wait()


def solution(mesh):
    spec = P(('batch', 'cy', 'cx'), None, None)

    def local(q, k, v):
        t, h, d = q.shape
        kvh = k.shape[1]
        gq = h // kvh
        ch = t // 2
        ndev = mesh.shape['cy'] * mesh.shape['cx']
        w = QT * gq
        rows = 9 * 2 * ch
        any_spec = pl.BlockSpec(memory_space=pltpu.HBM)
        operands = [pltpu.with_memory_space_constraint(x, pltpu.HBM) for x in (q.reshape(t, kvh, gq, d), k, v)]
        states = [
            jax.ShapeDtypeStruct((t, kvh, gq, d), jnp.bfloat16),
            jax.ShapeDtypeStruct((t, gq, d), jnp.bfloat16),
            jax.ShapeDtypeStruct((4, 2, ch, d), jnp.bfloat16),
            jax.ShapeDtypeStruct((2, NT, 1, w), jnp.float32),
            jax.ShapeDtypeStruct((2, NT, 1, w), jnp.float32),
            jax.ShapeDtypeStruct((2, NT, d, w), jnp.float32),
        ]
        vmem = pl.BlockSpec(memory_space=pltpu.VMEM)
        states = pl.pallas_call(
            functools.partial(kernel, scale=d ** -0.5),
            out_shape=states,
            in_specs=[any_spec] * 3,
            out_specs=[vmem] * 6,
            scratch_shapes=[
                pltpu.VMEM((kvh, t, gq, d), jnp.bfloat16),
                pltpu.VMEM((2, t, kvh, d), jnp.bfloat16),
                pltpu.VMEM((2, t * kvh, d), jnp.float32),
                pltpu.VMEM((kvh + 1, 2 * ndev, 2, ch, d), jnp.bfloat16),
                pltpu.VMEM((2, d, 12 * ch), jnp.bfloat16),
                pltpu.VMEM((2, d, 4 * ch), jnp.bfloat16),
                *[pltpu.VMEM((rows, w), jnp.float32)] * 3,
                *[pltpu.VMEM((rows, w), jnp.bfloat16)] * 3,
                *[pltpu.VMEM((4, 1, w), jnp.float32)] * 3,
                *[pltpu.VMEM((2, 1, w), jnp.float32)] * 6,
                *[pltpu.VMEM((4, 1, w), jnp.float32)] * 3,
                pltpu.SemaphoreType.DMA((3,)),
                *[pltpu.SemaphoreType.DMA((kvh,))] * 5,
            ],
            compiler_params=pltpu.CompilerParams(
                collective_id=0, has_side_effects=True, vmem_limit_bytes=40 * 2**20),
            name='ring_attention',
        )(*operands)
        out = pl.pallas_call(
            functools.partial(last_kernel, scale=d ** -0.5),
            out_shape=jax.ShapeDtypeStruct((t, kvh, gq, d), jnp.bfloat16),
            in_specs=[vmem] * 6,
            out_specs=any_spec,
            scratch_shapes=[
                pltpu.VMEM((t, gq, d), jnp.bfloat16),
                pltpu.VMEM((12 * ch, w), jnp.float32),
                pltpu.VMEM((12 * ch, w), jnp.bfloat16),
                pltpu.SemaphoreType.DMA((kvh + 3,)),
            ],
            compiler_params=pltpu.CompilerParams(vmem_limit_bytes=16 * 2**20),
            name='write_result',
        )(*states)
        return out.reshape(t, h, d)

    return jax.shard_map(local, mesh=mesh, in_specs=(spec, spec, spec), out_specs=spec, check_vma=False)
```

profile of v0, /device:TPU:0, one launch (start us, length us, event | category | flops | bytes accessed | tf_op | source)
XLA Modules:
  0.0 37.1 jit_solution(10698821935648003716)
XLA Ops:
  0.0 35.3 %ring_attention.1 = (bf16[192,8,8,128]{3,2,1,0:T(8,128)(2,1)S(1)}, bf16[192,8,128]{2,1,0:T(8,128)(2,1)S(1)}, bf16[4,2,96,128]{3,2,1,0:T(8,128)(2,1)S(1)}, f32[2,...) custom-call(bf16[192,8,8,128]{3,2,1,0:T(8,128)(2,1)} %bitcast.2, ...), custom_call_target="tpu_custom_call" | custom-call | tf_op jit(solution)/shard_map/ring_attention/pallas_call | solution.py:412
  35.3 1.8 %write_result.1 = bf16[192,8,8,128]{3,2,1,0:T(8,128)(2,1)} custom-call(bf16[192,8,8,128]{3,2,1,0:T(8,128)(2,1)S(1)} %get-tuple-element.11.o_part, bf16[192,8,128]{2,1,0:T(8,128)(2,1)S(1)} %get-tuple-element.12.q_last, bf16[4,2,96,128]{3,2,1,0:T(8,128)(2,1)S(1)} %get-tuple-element.13.kv_last, f32[2,3,1,256]{3,2,1,0:T(1,128)S(1)} %get-tuple-element.14.mk, ...), custom_call_target="tpu_custom_call" | custom-call | tf_op jit(solution)/shard_map/write_result/pallas_call | solution.py:436
where the time goes:
time: 37.2 us; the launch traced here: 37.1 us
  Pallas kernels  37.1 us (100%)
    pallas_call x1, Pallas kernels, local(): pl.pallas_call(functools.partial(kernel, scale=d ** (-0.5)), out_shape=st...  35.3 us
    pallas_call x1, Pallas kernels, local(): pl.pallas_call(functools.partial(last_kernel, scale=d ** (-0.5)), out_sha...  1.75 us

commit v1 on v0

--- a/solution.py
+++ b/solution.py
@@ -9,7 +9,7 @@
 from jax.sharding import PartitionSpec as P
 
 MESH = pl.DeviceIdType.MESH
-AHEAD = 2
+AHEAD = 3
 QT = 32
 NT = 3
 NEG = -jnp.inf
@@ -169,19 +169,20 @@
 
         def stage_a(u, slot, early=True, late=True):
             g, t = split(u)
-            gl = jnp.where(g == 0, G, g - 1)
-            ql = jnp.maximum(g - 1, 0)
+            par = lax.rem(g + 2, 2)
+            gl = jnp.where(g < 2, G, g - 2)
+            ql = jnp.maximum(g - 2, 0)
             for half in halves:
                 e, l = ('eh', 'lh') if half else ('el', 'll')
                 if late and lst[l]:
-                    old = mk[half, t]
+                    old = mk[par, half, t]
                     m = jnp.maximum(score_late(gl, ql, t, half, l, slot), old)
                     m_s[slot][2 + half] = m
                     al_s[slot][half] = jnp.exp2((old - m) * c2)
                 if early:
                     m = score(g, t, half, e, slot, True)
                     m_s[slot][half] = m
-                    mk[half, t] = m
+                    mk[par, half, t] = m
 
         def score_late(gl, ql, t, half, name, slot):
             at, n = rows[name]
@@ -208,16 +209,17 @@
 
         def stage_b(u, slot, early=True, late=True):
             g, t = split(u)
+            par = lax.rem(g + 2, 2)
             for half in halves:
                 e, l = ('eh', 'lh') if half else ('el', 'll')
                 if late and lst[l]:
                     total = weights(l, slot, m_s[slot][2 + half])
-                    l_s[slot][2 + half] = lk[half, t] * al_s[slot][half] + total
+                    l_s[slot][2 + half] = lk[par, half, t] * al_s[slot][half] + total
                     be_s[slot][half] = al_s[slot][half]
                 if early:
                     total = weights(e, slot, m_s[slot][half])
                     l_s[slot][half] = total
-                    lk[half, t] = total
+                    lk[par, half, t] = total
 
         def values(name, ref, par, slot):
             at, n = rows[name]
@@ -230,31 +232,28 @@
 
         def stage_c(u, slot, early=True, late=True):
             g, t = split(u)
+            par = lax.rem(g + 2, 2)
             ge = jnp.maximum(g, 0)
-            gl = jnp.maximum(g - 1, 0)
+            gl = jnp.maximum(g - 2, 0)
             for half in halves:
                 e, l = ('eh', 'lh') if half else ('el', 'll')
                 if late and lst[l]:
-                    acc = acck[half, t] * be_s[slot][half] + values(l, vtl, lax.rem(gl, 2), slot)
+                    acc = acck[par, half, t] * be_s[slot][half] + values(l, vtl, lax.rem(gl, 2), slot)
                     put(gl, t, half, acc, l_s[slot][2 + half])
                 if early:
                     acc = values(e, vte, lax.rem(ge, 2), slot)
                     if lst[l]:
-                        acck[half, t] = acc
+                        acck[par, half, t] = acc
                     else:
                         put(ge, t, half, acc, l_s[slot][half])
 
         def service(g):
-            @pl.when(g < G - 1)
+            arrived(g, 2 + n_xy, se_sem)
+
+            @pl.when(g > 1)
             def _():
-                forward(g + 1)
-
-            arrived(g, 2 + n_xy, se_sem)
-
-            @pl.when(g > 0)
-            def _():
-                arrived(g - 1, n_far, sl_sem)
-                transposed(g - 1, lax.rem(g - 1, 2), (('lh', vtl),))
+                arrived(g - 2, n_far, sl_sem)
+                transposed(g - 2, lax.rem(g, 2), (('lh', vtl),))
             transposed(g, lax.rem(g, 2), (('eh', vte),))
 
         n = NT * G
@@ -269,13 +268,17 @@
                 def _(i=i):
                     service(lax.div(i, NT))
 
+                @pl.when(jnp.logical_and(lax.rem(i, NT) == 1, i < n - NT))
+                def _(i=i):
+                    forward(lax.div(i, NT) + 1)
+
                 @pl.when(jnp.logical_and(lax.rem(i, NT) == 1, i < n - NT - NT * AHEAD))
                 def _(i=i):
                     start_own(lax.div(i, NT) + 1 + AHEAD)
 
-                @pl.when(jnp.logical_and(lax.rem(i, NT) == 1, i < n - NT))
+                @pl.when(jnp.logical_and(lax.rem(i, NT) == 2, i >= NT))
                 def _(i=i):
-                    diagonal(lax.div(i, NT))
+                    diagonal(lax.div(i, NT) - 1)
 
                 stage_a(i, odd_i)
                 stage_b(i - 1, 1 - odd_i)
@@ -287,6 +290,14 @@
         stage_c(n - 1, 1 - n % 2)
 
         diagonal(G - 1)
+        arrived(G - 2, n_far, sl_sem)
+        transposed(G - 2, G % 2, (('lh', vtl),))
+        for t in range(NT):
+            stage_a(n + t, t, early=False)
+        for t in range(NT):
+            stage_b(n + t, t, early=False)
+        for t in range(NT):
+            stage_c(n + t, t, early=False)
         arrived(G - 1, n_far, sl_sem)
         for i, (half, j) in enumerate(lst['lh']):
             for core in (0, 1):
@@ -300,14 +311,6 @@
             return carry
 
         lax.fori_loop(0, G, drain, 0)
-
-    def tail(stage_a, stage_b, stage_c, n):
-        for t in range(NT):
-            stage_a(n + t, t, early=False)
-        for t in range(NT):
-            stage_b(n + t, t, early=False)
-        for t in range(NT):
-            stage_c(n + t, t, early=False)
 
     for chip in range(4):
         @pl.when(chip_of == chip)
@@ -326,6 +329,7 @@
     for c in copies:
         c.start()
     c2 = scale * math.log2(math.e)
+    last = (G - 1) % 2
 
     def merge(chip):
         late_high, late_low = chunks_of(chip)[2:]
@@ -347,7 +351,7 @@
                                 preferred_element_type=jnp.float32)
             s_s[at:at + n] = s
             top = functools.reduce(jnp.maximum, slabs(s))
-            tops.append(jnp.maximum(jnp.max(top, axis=0, keepdims=True), mk[half, t]))
+            tops.append(jnp.maximum(jnp.max(top, axis=0, keepdims=True), mk[last, half, t]))
             at += n
         at = 0
         for (half, t, count), m in zip(tiles, tops):
@@ -365,9 +369,9 @@
         for (half, t, count), m, total in zip(tiles, tops, sums):
             n = 2 * CH * count
             rows = slice(half * CH + t * QT, half * CH + (t + 1) * QT)
-            alpha = jnp.exp2((mk[half, t] - m) * c2)
-            inv = 1.0 / (lk[half, t] * alpha + total)
-            acc = acck[half, t] * (alpha * inv) + lax.dot_general(
+            alpha = jnp.exp2((mk[last, half, t] - m) * c2)
+            inv = 1.0 / (lk[last, half, t] * alpha + total)
+            acc = acck[last, half, t] * (alpha * inv) + lax.dot_general(
                 vals[:, :n], p_s[at:at + n], (((1,), (0,)), ((), ())), preferred_element_type=jnp.float32) * inv
             out_s[rows] = acc.astype(jnp.bfloat16).T.reshape(QT, GQ, D)
             at += n
@@ -404,9 +408,9 @@
             jax.ShapeDtypeStruct((t, kvh, gq, d), jnp.bfloat16),
             jax.ShapeDtypeStruct((t, gq, d), jnp.bfloat16),
             jax.ShapeDtypeStruct((4, 2, ch, d), jnp.bfloat16),
-            jax.ShapeDtypeStruct((2, NT, 1, w), jnp.float32),
-            jax.ShapeDtypeStruct((2, NT, 1, w), jnp.float32),
-            jax.ShapeDtypeStruct((2, NT, d, w), jnp.float32),
+            jax.ShapeDtypeStruct((2, 2, NT, 1, w), jnp.float32),
+            jax.ShapeDtypeStruct((2, 2, NT, 1, w), jnp.float32),
+            jax.ShapeDtypeStruct((2, 2, NT, d, w), jnp.float32),
         ]
         vmem = pl.BlockSpec(memory_space=pltpu.VMEM)
         states = pl.pallas_call(

time: 37.2 us -> 36.3 us (0.976)
  Pallas kernels: 37.1 us -> 36.1 us
    pallas_call x1, Pallas kernels: 35.3 us -> 34.3 us  [local(): pl.pallas_call(functools.partial(kernel, scale=d ** (-0.5)), out_shape=st...]
where the time goes in v1:
time: 36.3 us
  Pallas kernels  36.1 us (99%)
    pallas_call x1, Pallas kernels, local(): pl.pallas_call(functools.partial(kernel, scale=d ** (-0.5)), out_shape=st...  34.3 us
    pallas_call x1, Pallas kernels, local(): pl.pallas_call(functools.partial(last_kernel, scale=d ** (-0.5)), out_sha...  1.75 us

profile of v1, /device:TPU:0, one launch (start us, length us, event | category | flops | bytes accessed | tf_op | source)
XLA Modules:
  0.0 36.3 jit_solution(12527849023291627678)
XLA Ops:
  0.0 34.3 %ring_attention.1 = (bf16[192,8,8,128]{3,2,1,0:T(8,128)(2,1)S(1)}, bf16[192,8,128]{2,1,0:T(8,128)(2,1)S(1)}, bf16[4,2,96,128]{3,2,1,0:T(8,128)(2,1)S(1)}, f32[2,...) custom-call(bf16[192,8,8,128]{3,2,1,0:T(8,128)(2,1)} %bitcast.2, ...), custom_call_target="tpu_custom_call" | custom-call | tf_op jit(solution)/shard_map/ring_attention/pallas_call | solution.py:416
  34.3 1.8 %write_result.1 = bf16[192,8,8,128]{3,2,1,0:T(8,128)(2,1)} custom-call(bf16[192,8,8,128]{3,2,1,0:T(8,128)(2,1)S(1)} %get-tuple-element.11.o_part, bf16[192,8,128]{2,1,0:T(8,128)(2,1)S(1)} %get-tuple-element.12.q_last, bf16[4,2,96,128]{3,2,1,0:T(8,128)(2,1)S(1)} %get-tuple-element.13.kv_last, f32[2,2,3,1,256]{4,3,2,1,0:T(1,128)S(1)} %get-tuple-element.14.mk, ...), custom_call_target="tpu_custom_call" | custom-call | tf_op jit(solution)/shard_map/write_result/pallas_call | solution.py:440

commit v2 on v1

--- a/solution.py
+++ b/solution.py
@@ -27,8 +27,8 @@
 
 def kernel(q_hbm, k_hbm, v_hbm, o_ref, q_last, kv_last, mk, lk, acck, q_s, raw, f32s, kv, vte, vtl, *rest,
            scale):
-    s_s, p_s, m_s, al_s, be_s, l_s = (rest[3 * i:3 * i + 3] for i in range(6))
-    load_sem, send_sem, xy_sem, dg_sem, se_sem, sl_sem = rest[18:]
+    s_s, p_s, m_s, al_s, be_s, l_s, fin_s = (rest[3 * i:3 * i + 3] for i in range(7))
+    load_sem, send_sem, xy_sem, dg_sem, se_sem, sl_sem = rest[21:]
     G, T, GQ, D = q_s.shape
     CH = T // 2
     C2 = 2 * CH
@@ -226,9 +226,16 @@
             return lax.dot_general(ref[par, :, :n], p_s[slot][at:at + n], (((1,), (0,)), ((), ())),
                                    preferred_element_type=jnp.float32)
 
-        def put(g, t, half, acc, total):
-            out = (acc * (1.0 / total)).astype(jnp.bfloat16).T
-            o_ref[pl.ds(half * CH + t * QT, QT), g] = out.reshape(QT, GQ, D)
+        def put(slot, half, acc, total):
+            fin_s[slot][half] = (acc * (1.0 / total)).astype(jnp.bfloat16)
+
+        def stage_d(u, slot, late_only=False):
+            g, t = split(u)
+            for half in halves:
+                late = bool(lst['lh' if half else 'll'])
+                if late or not late_only:
+                    to = jnp.maximum(g - 2, 0) if late else jnp.maximum(g, 0)
+                    o_ref[pl.ds(half * CH + t * QT, QT), to] = fin_s[slot][half].T.reshape(QT, GQ, D)
 
         def stage_c(u, slot, early=True, late=True):
             g, t = split(u)
@@ -239,13 +246,13 @@
                 e, l = ('eh', 'lh') if half else ('el', 'll')
                 if late and lst[l]:
                     acc = acck[par, half, t] * be_s[slot][half] + values(l, vtl, lax.rem(gl, 2), slot)
-                    put(gl, t, half, acc, l_s[slot][2 + half])
+                    put(slot, half, acc, l_s[slot][2 + half])
                 if early:
                     acc = values(e, vte, lax.rem(ge, 2), slot)
                     if lst[l]:
                         acck[par, half, t] = acc
                     else:
-                        put(ge, t, half, acc, l_s[slot][half])
+                        put(slot, half, acc, l_s[slot][half])
 
         def service(g):
             arrived(g, 2 + n_xy, se_sem)
@@ -283,13 +290,16 @@
                 stage_a(i, odd_i)
                 stage_b(i - 1, 1 - odd_i)
                 stage_c(i - 1, 1 - odd_i)
+                stage_d(i - 2, odd_i)
             return carry
 
         lax.fori_loop(0, n // 2, body, 0)
+        diagonal(G - 1)
         stage_b(n - 1, 1 - n % 2)
         stage_c(n - 1, 1 - n % 2)
-
-        diagonal(G - 1)
+        stage_d(n - 2, n % 2)
+        stage_d(n - 1, 1 - n % 2)
+
         arrived(G - 2, n_far, sl_sem)
         transposed(G - 2, G % 2, (('lh', vtl),))
         for t in range(NT):
@@ -298,6 +308,7 @@
             stage_b(n + t, t, early=False)
         for t in range(NT):
             stage_c(n + t, t, early=False)
+            stage_d(n + t, t, late_only=True)
         arrived(G - 1, n_far, sl_sem)
         for i, (half, j) in enumerate(lst['lh']):
             for core in (0, 1):
@@ -430,6 +441,7 @@
                 *[pltpu.VMEM((4, 1, w), jnp.float32)] * 3,
                 *[pltpu.VMEM((2, 1, w), jnp.float32)] * 6,
                 *[pltpu.VMEM((4, 1, w), jnp.float32)] * 3,
+                *[pltpu.VMEM((2, d, w), jnp.bfloat16)] * 3,
                 pltpu.SemaphoreType.DMA((3,)),
                 *[pltpu.SemaphoreType.DMA((kvh,))] * 5,
             ],

time: 36.3 us -> 36.1 us (level)
  no operation moved by 1% of the time
where the time goes in v2:
time: 36.1 us; the launch traced here: 36 us
  Pallas kernels  35.8 us (99%)
    pallas_call x1, Pallas kernels, local(): pl.pallas_call(functools.partial(kernel, scale=d ** (-0.5)), out_shape=st...  34.1 us
    pallas_call x1, Pallas kernels, local(): pl.pallas_call(functools.partial(last_kernel, scale=d ** (-0.5)), out_sha...  1.75 us

profile of v2, /device:TPU:0, one launch (start us, length us, event | category | flops | bytes accessed | tf_op | source)
XLA Modules:
  0.0 36.0 jit_solution(5059318859635942086)
XLA Ops:
  0.0 34.1 %ring_attention.1 = (bf16[192,8,8,128]{3,2,1,0:T(8,128)(2,1)S(1)}, bf16[192,8,128]{2,1,0:T(8,128)(2,1)S(1)}, bf16[4,2,96,128]{3,2,1,0:T(8,128)(2,1)S(1)}, f32[2,...) custom-call(bf16[192,8,8,128]{3,2,1,0:T(8,128)(2,1)} %bitcast.2, ...), custom_call_target="tpu_custom_call" | custom-call | tf_op jit(solution)/shard_map/ring_attention/pallas_call | solution.py:427
  34.1 1.8 %write_result.1 = bf16[192,8,8,128]{3,2,1,0:T(8,128)(2,1)} custom-call(bf16[192,8,8,128]{3,2,1,0:T(8,128)(2,1)S(1)} %get-tuple-element.11.o_part, bf16[192,8,128]{2,1,0:T(8,128)(2,1)S(1)} %get-tuple-element.12.q_last, bf16[4,2,96,128]{3,2,1,0:T(8,128)(2,1)S(1)} %get-tuple-element.13.kv_last, f32[2,2,3,1,256]{4,3,2,1,0:T(1,128)S(1)} %get-tuple-element.14.mk, ...), custom_call_target="tpu_custom_call" | custom-call | tf_op jit(solution)/shard_map/write_result/pallas_call | solution.py:452

commit v3 on v2

--- a/solution.py
+++ b/solution.py
@@ -78,13 +78,13 @@
 
     def send(g, ref, recv_sem, dev):
         pltpu.make_async_remote_copy(
-            src_ref=ref, dst_ref=ref, send_sem=send_sem.at[g], recv_sem=recv_sem.at[g],
+            src_ref=ref, dst_ref=ref, send_sem=send_sem.at[0], recv_sem=recv_sem.at[g],
             device_id=dev, device_id_type=MESH).start()
 
     def arrived(g, count, recv_sem):
         ref = kv.at[g, 0:count]
         pltpu.make_async_remote_copy(
-            src_ref=ref, dst_ref=ref, send_sem=send_sem.at[g], recv_sem=recv_sem.at[g],
+            src_ref=ref, dst_ref=ref, send_sem=send_sem.at[0], recv_sem=recv_sem.at[g],
             device_id=x_dev, device_id_type=MESH).wait_recv()
 
     c2 = scale * math.log2(math.e)
@@ -279,7 +279,7 @@
                 def _(i=i):
                     forward(lax.div(i, NT) + 1)
 
-                @pl.when(jnp.logical_and(lax.rem(i, NT) == 1, i < n - NT - NT * AHEAD))
+                @pl.when(jnp.logical_and(lax.rem(i, NT) == 2, i < n - NT - NT * AHEAD))
                 def _(i=i):
                     start_own(lax.div(i, NT) + 1 + AHEAD)
 
@@ -314,14 +314,10 @@
             for core in (0, 1):
                 kv_last[2 * i + core] = kv[G - 1, 4 * j + half + 2 * core]
 
-        def drain(g, carry):
-            ref = kv.at[g, 0:n_sent]
-            pltpu.make_async_remote_copy(
-                src_ref=ref, dst_ref=ref, send_sem=send_sem.at[g], recv_sem=xy_sem.at[g],
-                device_id=x_dev, device_id_type=MESH).wait_send()
-            return carry
-
-        lax.fori_loop(0, G, drain, 0)
+        ref = kv.at[0:G, 0:n_sent]
+        pltpu.make_async_remote_copy(
+            src_ref=ref, dst_ref=ref, send_sem=send_sem.at[0], recv_sem=xy_sem.at[0],
+            device_id=x_dev, device_id_type=MESH).wait_send()
 
     for chip in range(4):
         @pl.when(chip_of == chip)
@@ -443,7 +439,8 @@
                 *[pltpu.VMEM((4, 1, w), jnp.float32)] * 3,
                 *[pltpu.VMEM((2, d, w), jnp.bfloat16)] * 3,
                 pltpu.SemaphoreType.DMA((3,)),
-                *[pltpu.SemaphoreType.DMA((kvh,))] * 5,
+                pltpu.SemaphoreType.DMA((1,)),
+                *[pltpu.SemaphoreType.DMA((kvh,))] * 4,
             ],
             compiler_params=pltpu.CompilerParams(
                 collective_id=0, has_side_effects=True, vmem_limit_bytes=40 * 2**20),

time: 36.1 us -> 36 us (level)
  no operation moved by 1% of the time
where the time goes in v3:
time: 36 us; the launch traced here: 35.9 us
  Pallas kernels  35.7 us (99%)
    pallas_call x1, Pallas kernels, local(): pl.pallas_call(functools.partial(kernel, scale=d ** (-0.5)), out_shape=st...  34 us
    pallas_call x1, Pallas kernels, local(): pl.pallas_call(functools.partial(last_kernel, scale=d ** (-0.5)), out_sha...  1.75 us

profile of v3, /device:TPU:0, one launch (start us, length us, event | category | flops | bytes accessed | tf_op | source)
XLA Modules:
  0.0 35.9 jit_solution(7461971870890511411)
XLA Ops:
  0.0 34.0 %ring_attention.1 = (bf16[192,8,8,128]{3,2,1,0:T(8,128)(2,1)S(1)}, bf16[192,8,128]{2,1,0:T(8,128)(2,1)S(1)}, bf16[4,2,96,128]{3,2,1,0:T(8,128)(2,1)S(1)}, f32[2,...) custom-call(bf16[192,8,8,128]{3,2,1,0:T(8,128)(2,1)} %bitcast.2, ...), custom_call_target="tpu_custom_call" | custom-call | tf_op jit(solution)/shard_map/ring_attention/pallas_call | solution.py:423
  34.0 1.8 %write_result.1 = bf16[192,8,8,128]{3,2,1,0:T(8,128)(2,1)} custom-call(bf16[192,8,8,128]{3,2,1,0:T(8,128)(2,1)S(1)} %get-tuple-element.11.o_part, bf16[192,8,128]{2,1,0:T(8,128)(2,1)S(1)} %get-tuple-element.12.q_last, bf16[4,2,96,128]{3,2,1,0:T(8,128)(2,1)S(1)} %get-tuple-element.13.kv_last, f32[2,2,3,1,256]{4,3,2,1,0:T(1,128)S(1)} %get-tuple-element.14.mk, ...), custom_call_target="tpu_custom_call" | custom-call | tf_op jit(solution)/shard_map/write_result/pallas_call | solution.py:449

commit v4 on v3

--- a/solution.py
+++ b/solution.py
@@ -330,9 +330,9 @@
     CH = T // 2
     W = QT * GQ
     chip_of = lax.axis_index('cy') * 2 + lax.axis_index('cx') // 2
-    step = T // 4
+    step = T
     copies = [pltpu.make_async_copy(o_part.at[pl.ds(i * step, step), pl.ds(0, G - 1)],
-                                    o_hbm.at[pl.ds(i * step, step), pl.ds(0, G - 1)], sem.at[i]) for i in range(4)]
+                                    o_hbm.at[pl.ds(i * step, step), pl.ds(0, G - 1)], sem.at[i]) for i in range(1)]
     for c in copies:
         c.start()
     c2 = scale * math.log2(math.e)
@@ -344,7 +344,7 @@
         tiles += [(0, t, len(late_low)) for t in range(NT) if late_low]
         ends = []
         if not late_low:
-            ends.append(pltpu.make_async_copy(o_part.at[pl.ds(0, CH), G - 1], o_hbm.at[pl.ds(0, CH), G - 1], sem.at[G]))
+            ends.append(pltpu.make_async_copy(o_part.at[pl.ds(0, CH), G - 1], o_hbm.at[pl.ds(0, CH), G - 1], sem.at[1]))
             ends[0].start()
         n_pieces = 2 * len(late_high)
         keys = kv_last[0:n_pieces, 0].reshape(n_pieces * CH, D)
@@ -384,7 +384,7 @@
             at += n
         for half in ((1, 0) if late_low else (1,)):
             ends.append(pltpu.make_async_copy(
-                out_s.at[pl.ds(half * CH, CH)], o_hbm.at[pl.ds(half * CH, CH), G - 1], sem.at[G + 1 + half]))
+                out_s.at[pl.ds(half * CH, CH)], o_hbm.at[pl.ds(half * CH, CH), G - 1], sem.at[2 + half]))
             ends[-1].start()
         for c in ends:
             c.wait()
@@ -455,7 +455,7 @@
                 pltpu.VMEM((t, gq, d), jnp.bfloat16),
                 pltpu.VMEM((12 * ch, w), jnp.float32),
                 pltpu.VMEM((12 * ch, w), jnp.bfloat16),
-                pltpu.SemaphoreType.DMA((kvh + 3,)),
+                pltpu.SemaphoreType.DMA((4,)),
             ],
             compiler_params=pltpu.CompilerParams(vmem_limit_bytes=16 * 2**20),
             name='write_result',

time: 36 us -> 35.9 us (level)
  no operation moved by 1% of the time
where the time goes in v4:
time: 35.9 us; the launch traced here: 35.8 us
  Pallas kernels  35.6 us (99%)
    pallas_call x1, Pallas kernels, local(): pl.pallas_call(functools.partial(kernel, scale=d ** (-0.5)), out_shape=st...  34 us
    pallas_call x1, Pallas kernels, local(): pl.pallas_call(functools.partial(last_kernel, scale=d ** (-0.5)), out_sha...  1.69 us

profile of v4, /device:TPU:0, one launch (start us, length us, event | category | flops | bytes accessed | tf_op | source)
XLA Modules:
  0.0 35.8 jit_solution(15241104899608829574)
XLA Ops:
  0.0 34.0 %ring_attention.1 = (bf16[192,8,8,128]{3,2,1,0:T(8,128)(2,1)S(1)}, bf16[192,8,128]{2,1,0:T(8,128)(2,1)S(1)}, bf16[4,2,96,128]{3,2,1,0:T(8,128)(2,1)S(1)}, f32[2,...) custom-call(bf16[192,8,8,128]{3,2,1,0:T(8,128)(2,1)} %bitcast.2, ...), custom_call_target="tpu_custom_call" | custom-call | tf_op jit(solution)/shard_map/ring_attention/pallas_call | solution.py:423
  34.0 1.7 %write_result.1 = bf16[192,8,8,128]{3,2,1,0:T(8,128)(2,1)} custom-call(bf16[192,8,8,128]{3,2,1,0:T(8,128)(2,1)S(1)} %get-tuple-element.11.o_part, bf16[192,8,128]{2,1,0:T(8,128)(2,1)S(1)} %get-tuple-element.12.q_last, bf16[4,2,96,128]{3,2,1,0:T(8,128)(2,1)S(1)} %get-tuple-element.13.kv_last, f32[2,2,3,1,256]{4,3,2,1,0:T(1,128)S(1)} %get-tuple-element.14.mk, ...), custom_call_target="tpu_custom_call" | custom-call | tf_op jit(solution)/shard_map/write_result/pallas_call | solution.py:449
